TPU v7x, 32 devices: a whole 2x2x4 slice. The times are simulated.
32 devices in a mesh: dev: 32 (over z, y, x, core).
Axes of the slice: x: 2, y: 2, z: 4, core: 2. Of those that a mesh axis runs over, the one named last changes fastest.
Arguments:
- tokens: bfloat16 [4608, 1536], P('dev'), may hold values from -6 to 6
- conditioning: bfloat16 [4, 1536], replicated, may hold values from -5 to 5
- text_lengths: int32 [4], replicated, may hold values from 86 to 154, as said below
- modulation_weight: bfloat16 [3072, 9216], P('dev'), may hold values from -0.15625 to 0.15625
- project_weight: bfloat16 [3072, 4608], P('dev'), may hold values from -1 to 1
- merge_weight: bfloat16 [3072, 1536], P('dev'), may hold values from -1.25 to 1.25
- up_weight: bfloat16 [3072, 6144], P('dev'), may hold values from -0.15625 to 0.15625
- down_weight: bfloat16 [12288, 1536], P('dev'), may hold values from -0.078125 to 0.078125
- cotangent: bfloat16 [4608, 1536], P('dev'), may hold values from -6 to 6
Outputs:
- layer_out: bfloat16 [4608, 1536], P('dev')
- tokens_grad: float32 [4608, 1536], P('dev')
- conditioning_grad: float32 [4, 1536], replicated
- modulation_grad: float32 [3072, 9216], P('dev')
- project_grad: float32 [3072, 4608], P('dev')
- merge_grad: float32 [3072, 1536], P('dev')
- up_grad: float32 [3072, 6144], P('dev')
- down_grad: float32 [12288, 1536], P('dev')
Inputs may be any that keep to these rules, and one draw needn't show every extreme that they name: `text_lengths`: the text tokens of all sequences sum to 512, so that the sequences fill the packed rows exactly; one sequence has exactly 154 text tokens.
All inputs are finite; a program needn't handle non-finite values.
Results may differ from a plain program's by a relative error of at most 0.025.
The roundings to bfloat16 on the way count: a program that leaves them out, or rounds other values in their place, can miss the bound.
Values may be sent and summed in bfloat16 or wider, within the bound.
A program may use at most 576 MiB of HBM per device.

v0:
```python
import jax
import jax.numpy as jnp
from jax import lax
from jax.sharding import PartitionSpec as P

HEADS = 24
HDIM = 64
IMG = 1024
REACH = 9
TXT_CAP = 144


HIGHEST_PRECISION = lax.Precision.HIGHEST
EPSILON = 1e-06
CONTRACT_LAST = (((1,), (1,)), ((), ()))
CONTRACT_FIRST = (((0,), (0,)), ((), ()))


def passed_along(x, axis, by):
    length = lax.axis_size(axis)
    pairs = [(i, i + by) for i in range(length) if 0 <= i + by < length]
    return lax.ppermute(x, axis, pairs)


def layer_norm(values):
    mean = jnp.mean(values, axis=-1, keepdims=True)
    centred = values - mean
    variance = jnp.mean(centred * centred, axis=-1, keepdims=True)
    inv_std = lax.rsqrt(variance + EPSILON)
    return (centred * inv_std, inv_std)


def norm_back(grad_normed, normed, inv_std):
    mean_grad = jnp.mean(grad_normed, axis=-1, keepdims=True)
    mean_cross = jnp.mean(grad_normed * normed, axis=-1, keepdims=True)
    return inv_std * (grad_normed - mean_grad - normed * mean_cross)


def sequence_index(positions, starts):
    return jnp.sum((starts[None, :] <= positions[:, None]).astype(jnp.int32), axis=1) - 1


def stream_dot(rows, stacked, layout):
    text_rows, text_valid, slot_of_row, is_text = layout
    half = stacked.shape[0] // 2
    image_part = jnp.dot(rows, stacked[:half], preferred_element_type=jnp.float32)
    text_part = jnp.dot(rows[text_rows], stacked[half:], preferred_element_type=jnp.float32)
    return jnp.where(is_text[:, None], text_part[slot_of_row], image_part)


def stream_rows_back(stacked, grad_low, layout):
    text_rows, text_valid, slot_of_row, is_text = layout
    half = stacked.shape[0] // 2
    image_grad = jnp.where(is_text[:, None], jnp.zeros_like(grad_low), grad_low)
    picked = grad_low[text_rows]
    text_grad = jnp.where(text_valid[:, None], picked, jnp.zeros_like(picked))
    image_back = lax.dot_general(
        image_grad, stacked[:half], CONTRACT_LAST, preferred_element_type=jnp.float32
    )
    text_back = lax.dot_general(
        text_grad, stacked[half:], CONTRACT_LAST, preferred_element_type=jnp.float32
    )
    return jnp.where(is_text[:, None], text_back[slot_of_row], image_back)


def split_streams(rows, is_text):
    zeros = jnp.zeros_like(rows)
    return jnp.concatenate(
        [jnp.where(is_text[:, None], zeros, rows), jnp.where(is_text[:, None], rows, zeros)], axis=1
    )


def term_rows(stacked_rows, grad_low):
    return lax.dot_general(
        stacked_rows, grad_low, CONTRACT_FIRST, preferred_element_type=jnp.float32
    )


def gather_tail(merge_weight, up_weight, down_weight):
    return (
        lax.all_gather(merge_weight, "dev", axis=0, tiled=True),
        lax.all_gather(up_weight, "dev", axis=0, tiled=True),
        lax.all_gather(down_weight, "dev", axis=0, tiled=True),
    )


def heads_last(stacked, count):
    return jnp.transpose(stacked, (1, 0, 2)).reshape(count, HEADS * HDIM)


def on_device(
    tokens,
    conditioning,
    text_lengths,
    modulation_weight,
    project_weight,
    merge_weight,
    up_weight,
    down_weight,
    cotangent,
):
    rows_dev = tokens.shape[0]
    width = tokens.shape[1]
    shard_rows = modulation_weight.shape[0]
    seq_count = conditioning.shape[0]
    devices = lax.axis_size("dev")
    device = lax.axis_index("dev")
    window = (2 * REACH + 1) * rows_dev
    scale = HDIM ** (-0.5)
    own_stream = device * shard_rows // width
    feature_start = device * shard_rows % width
    lengths = IMG + text_lengths
    ends = jnp.cumsum(lengths)
    starts = jnp.concatenate([jnp.zeros((1,), jnp.int32), ends[:-1]])
    positions = device * rows_dev + jnp.arange(rows_dev, dtype=jnp.int32)
    row_seq = sequence_index(positions, starts)
    row_start = jnp.max(
        jnp.where(starts[None, :] <= positions[:, None], starts[None, :], 0), axis=1
    )
    is_text = positions - row_start >= IMG
    text_count = jnp.cumsum(is_text.astype(jnp.int32))
    slot_of_row = jnp.clip(text_count - 1, 0, TXT_CAP - 1)
    slot_range = jnp.arange(TXT_CAP, dtype=jnp.int32)
    text_rows = jnp.clip(
        jnp.sum((text_count[None, :] <= slot_range[:, None]).astype(jnp.int32), axis=1),
        0,
        rows_dev - 1,
    )
    text_valid = slot_range < text_count[-1]
    layout = (text_rows, text_valid, slot_of_row, is_text)
    codes = row_seq * 2 + is_text.astype(jnp.int32)
    one_hot = (codes[:, None] == jnp.arange(2 * seq_count, dtype=jnp.int32)[None, :]).astype(
        jnp.float32
    )
    key_positions = device * rows_dev - REACH * rows_dev + jnp.arange(window, dtype=jnp.int32)
    key_valid = (key_positions >= 0) & (key_positions < devices * rows_dev)
    key_seq = sequence_index(key_positions, starts)
    mask = (row_seq[:, None] == key_seq[None, :]) & key_valid[None, :]
    cond_float = conditioning.astype(jnp.float32)
    silu_low = jax.nn.silu(cond_float).astype(jnp.bfloat16)
    silu_part = lax.dynamic_slice_in_dim(silu_low, feature_start, shard_rows, 1)
    mod_full, project_full = (
        lax.all_gather(modulation_weight, "dev", axis=0, tiled=True),
        lax.all_gather(project_weight, "dev", axis=0, tiled=True),
    )
    mod_table = jnp.einsum(
        "sd,jdc->sjc",
        silu_low,
        mod_full.reshape(2, width, 6 * width),
        preferred_element_type=jnp.float32,
    )
    mod_rows = jnp.dot(
        one_hot,
        mod_table.reshape(2 * seq_count, 6 * width),
        precision=HIGHEST_PRECISION,
        preferred_element_type=jnp.float32,
    )
    shift_a, scale_a, gate_a, shift_b, scale_b, gate_b = jnp.split(mod_rows, 6, axis=1)
    inputs = tokens.astype(jnp.float32)
    normed_a, inv_a = layer_norm(inputs)
    hidden_a = (normed_a * (1.0 + scale_a) + shift_a).astype(jnp.bfloat16)
    projected = stream_dot(hidden_a, project_full, layout).astype(jnp.bfloat16)
    queries, keys, values = jnp.split(projected, 3, axis=1)
    key_pieces = []
    value_pieces = []
    for offset in range(-REACH, REACH + 1):
        if offset == 0:
            key_pieces.append(keys)
            value_pieces.append(values)
        else:
            got_keys, got_values = passed_along((keys, values), "dev", -offset)
            key_pieces.append(got_keys)
            value_pieces.append(got_values)
    window_keys = jnp.concatenate(key_pieces, axis=0)
    window_values = jnp.concatenate(value_pieces, axis=0)

    def head_forward(head):
        query = lax.dynamic_slice_in_dim(queries, head * HDIM, HDIM, 1)
        key_cols = lax.dynamic_slice_in_dim(window_keys, head * HDIM, HDIM, 1)
        value_cols = lax.dynamic_slice_in_dim(window_values, head * HDIM, HDIM, 1)
        scores = (
            lax.dot_general(query, key_cols, CONTRACT_LAST, preferred_element_type=jnp.float32)
            * scale
        )
        masked = jnp.where(mask, scores, -jnp.inf)
        top = jnp.max(masked, axis=1, keepdims=True)
        exponent = jnp.exp(masked - top)
        total = jnp.sum(exponent, axis=1, keepdims=True)
        probs = (exponent / total).astype(jnp.bfloat16)
        attended_head = jnp.dot(probs, value_cols, preferred_element_type=jnp.float32)
        return (attended_head, (top + jnp.log(total))[:, 0])

    head_out, log_totals = lax.map(head_forward, jnp.arange(HEADS, dtype=jnp.int32))
    attended = heads_last(head_out, rows_dev).astype(jnp.bfloat16)
    merge_full, up_full, down_full = gather_tail(merge_weight, up_weight, down_weight)
    merged = stream_dot(attended, merge_full, layout)
    middle = inputs + gate_a * merged
    normed_b, inv_b = layer_norm(middle)
    hidden_b = (normed_b * (1.0 + scale_b) + shift_b).astype(jnp.bfloat16)
    upper = stream_dot(hidden_b, up_full, layout)
    activated = jax.nn.gelu(upper, approximate=True).astype(jnp.bfloat16)
    lowered = stream_dot(activated, down_full, layout)
    layer_out = (middle + gate_b * lowered).astype(jnp.bfloat16)
    grad_out = cotangent.astype(jnp.float32)
    grad_gate_b = grad_out * lowered
    grad_lowered = (gate_b * grad_out).astype(jnp.bfloat16)
    merge_again, up_again, down_again = gather_tail(merge_weight, up_weight, down_weight)
    grad_activated = stream_rows_back(down_again, grad_lowered, layout)
    activated_split = split_streams(activated, is_text)
    down_grad = lax.psum_scatter(
        term_rows(activated_split, grad_lowered), "dev", scatter_dimension=0, tiled=True
    )
    gelu_pull = jax.vjp(lambda value_in: jax.nn.gelu(value_in, approximate=True), upper)[1]
    grad_upper = gelu_pull(grad_activated)[0].astype(jnp.bfloat16)
    grad_hidden_b = stream_rows_back(up_again, grad_upper, layout)
    grad_scale_b = grad_hidden_b * normed_b
    grad_middle = grad_out + norm_back(grad_hidden_b * (1.0 + scale_b), normed_b, inv_b)
    grad_gate_a = grad_middle * merged
    grad_merged = (gate_a * grad_middle).astype(jnp.bfloat16)
    grad_attended = stream_rows_back(merge_again, grad_merged, layout).astype(jnp.bfloat16)
    attended_split = split_streams(attended, is_text)
    hidden_b_split = split_streams(hidden_b, is_text)

    def head_backward(head):
        query = lax.dynamic_slice_in_dim(queries, head * HDIM, HDIM, 1)
        key_cols = lax.dynamic_slice_in_dim(window_keys, head * HDIM, HDIM, 1)
        value_cols = lax.dynamic_slice_in_dim(window_values, head * HDIM, HDIM, 1)
        grad_head = lax.dynamic_slice_in_dim(grad_attended, head * HDIM, HDIM, 1)
        log_total = log_totals[head]
        scores = (
            lax.dot_general(query, key_cols, CONTRACT_LAST, preferred_element_type=jnp.float32)
            * scale
        )
        probs = jnp.where(mask, jnp.exp(scores - log_total[:, None]), 0.0)
        grad_probs = lax.dot_general(
            grad_head, value_cols, CONTRACT_LAST, preferred_element_type=jnp.float32
        )
        inner = jnp.sum(probs * grad_probs, axis=1, keepdims=True)
        grad_scores = (probs * (grad_probs - inner)).astype(jnp.bfloat16)
        grad_query = jnp.dot(grad_scores, key_cols, preferred_element_type=jnp.float32) * scale
        grad_key = (
            lax.dot_general(grad_scores, query, CONTRACT_FIRST, preferred_element_type=jnp.float32)
            * scale
        )
        grad_value = lax.dot_general(
            probs.astype(jnp.bfloat16),
            grad_head,
            CONTRACT_FIRST,
            preferred_element_type=jnp.float32,
        )
        return (grad_query, grad_key, grad_value)

    head_queries, head_keys, head_values = lax.map(
        head_backward, jnp.arange(HEADS, dtype=jnp.int32)
    )
    grad_queries = heads_last(head_queries, rows_dev)
    grad_keys = heads_last(head_keys, window)
    grad_values = heads_last(head_values, window)
    centre = REACH * rows_dev
    key_total = grad_keys[centre : centre + rows_dev]
    value_total = grad_values[centre : centre + rows_dev]
    for offset in range(-REACH, REACH + 1):
        if offset != 0:
            block = (offset + REACH) * rows_dev
            got_key, got_value = (
                passed_along(
                    grad_keys[block : block + rows_dev].astype(jnp.bfloat16), "dev", offset
                ).astype(jnp.float32),
                passed_along(
                    grad_values[block : block + rows_dev].astype(jnp.bfloat16), "dev", offset
                ).astype(jnp.float32),
            )
            key_total = key_total + got_key
            value_total = value_total + got_value
    grad_projected = jnp.concatenate([grad_queries, key_total, value_total], axis=1).astype(
        jnp.bfloat16
    )
    project_again = lax.all_gather(project_weight, "dev", axis=0, tiled=True)
    grad_hidden_a = stream_rows_back(project_again, grad_projected, layout)
    hidden_a_split = split_streams(hidden_a, is_text)
    summed = lax.psum_scatter(
        jnp.concatenate(
            [
                term_rows(attended_split, grad_merged),
                term_rows(hidden_b_split, grad_upper),
                term_rows(hidden_a_split, grad_projected),
            ],
            axis=1,
        ),
        "dev",
        scatter_dimension=0,
        tiled=True,
    )
    merge_grad = summed[:, :width]
    up_grad = summed[:, width : width + up_weight.shape[1]]
    project_grad = summed[:, width + up_weight.shape[1] :]
    grad_scale_a = grad_hidden_a * normed_a
    tokens_grad = grad_middle + norm_back(grad_hidden_a * (1.0 + scale_a), normed_a, inv_a)
    grad_mod_rows = jnp.concatenate(
        [grad_hidden_a, grad_scale_a, grad_gate_a, grad_hidden_b, grad_scale_b, grad_gate_b], axis=1
    )
    local_table = lax.dot_general(
        one_hot,
        grad_mod_rows,
        CONTRACT_FIRST,
        precision=HIGHEST_PRECISION,
        preferred_element_type=jnp.float32,
    )
    grad_table = lax.psum(local_table.reshape(seq_count, 2, 6 * width), "dev").astype(jnp.bfloat16)
    own_grads = lax.dynamic_index_in_dim(grad_table, own_stream, 1, keepdims=False)
    modulation_grad = lax.dot_general(
        silu_part, own_grads, CONTRACT_FIRST, preferred_element_type=jnp.float32
    )
    grad_piece = lax.dot_general(
        own_grads, modulation_weight, CONTRACT_LAST, preferred_element_type=jnp.float32
    )
    gathered = lax.all_gather(grad_piece, "dev", axis=1, tiled=True)
    grad_silu = gathered[:, :width] + gathered[:, width:]
    silu_pull = jax.vjp(jax.nn.silu, cond_float)[1]
    conditioning_grad = silu_pull(grad_silu)[0]
    return (
        layer_out,
        tokens_grad,
        conditioning_grad,
        modulation_grad,
        project_grad,
        merge_grad,
        up_grad,
        down_grad,
    )


def solution(mesh):
    return jax.shard_map(
        on_device,
        mesh=mesh,
        in_specs=(
            P("dev", None),
            P(),
            P(),
            P("dev", None),
            P("dev", None),
            P("dev", None),
            P("dev", None),
            P("dev", None),
            P("dev", None),
        ),
        out_specs=(
            P("dev", None),
            P("dev", None),
            P(),
            P("dev", None),
            P("dev", None),
            P("dev", None),
            P("dev", None),
            P("dev", None),
        ),
        check_vma=False,
    )
```

profile of v0, /device:TPU:0, one launch (start us, length us, event | category | flops | bytes accessed | tf_op | source)
XLA Modules:
  0.0 4157.8 jit_solution(7847232623532628059)
XLA Ops:
  13.0 305.7 %all-gather.7.cloned.1.call-done = bf16[3072,9216]{1,0:T(8,128)(2,1)} async-done(((bf16[96,9216]{1,0:T(8,128)(2,1)}), bf16[3072,9216]{1,0:T(8,128)(2,1)}) %all-gather.7.cloned.1.call-update) | async-done | bytes 56623120 | tf_op jit(solution)/shard_map/all_gather | solution.py:143
  318.6 20.9 fusion.179
  346.8 142.1 %all-gather.9.cloned.1.call-done = bf16[3072,4608]{1,0:T(8,128)(2,1)} async-done(((bf16[96,4608]{1,0:T(8,128)(2,1)}), bf16[3072,4608]{1,0:T(8,128)(2,1)}) %all-gather.9.cloned.1.call-update) | async-done | bytes 28311568 | tf_op jit(solution)/shard_map/all_gather | solution.py:144
  524.7 14.7 collective-permute-done.18
  554.4 16.0 collective-permute-start.4
  623.6 24.8 collective-permute-start.19
  648.4 26.0 collective-permute-start.20
  674.5 20.2 collective-permute-start.21
  696.1 18.1 collective-permute-done.21
  714.3 20.5 collective-permute-start.23
  746.6 14.5 collective-permute-start.26
  776.2 70.4 %collective-permute-done.29 = bf16[144,1536]{1,0:T(8,128)(2,1)S(1)} collective-permute-done((bf16[144,1536]{1,0:T(8,128)(2,1)S(1)}, bf16[144,1536]{1,0:T(8,128)(2,1)S(1)}, u32[]{:S(2)}, u32[]{:S(2)}) %collective-permute-start.29) | collective-permute-done | bytes 442400 | tf_op jit(solution)/shard_map/ppermute | solution.py:22
  856.6 32.9 collective-permute-done.31
  898.5 69.9 %collective-permute-done.10 = bf16[144,1536]{1,0:T(8,128)(2,1)S(1)} collective-permute-done((bf16[144,1536]{1,0:T(8,128)(2,1)S(1)}, bf16[144,1536]{1,0:T(8,128)(2,1)S(1)}, u32[]{:S(2)}, u32[]{:S(2)}) %collective-permute-start.10) | collective-permute-done | bytes 442400 | tf_op jit(solution)/shard_map/ppermute | solution.py:22
  979.9 58.0 %collective-permute-done.13 = bf16[144,1536]{1,0:T(8,128)(2,1)S(1)} collective-permute-done((bf16[144,1536]{1,0:T(8,128)(2,1)S(1)}, bf16[144,1536]{1,0:T(8,128)(2,1)S(1)}, u32[]{:S(2)}, u32[]{:S(2)}) %collective-permute-start.13) | collective-permute-done | bytes 442400 | tf_op jit(solution)/shard_map/ppermute | solution.py:22
  1038.0 18.6 collective-permute-done.14
  1060.0 164.2 %while.28 = (s32[]{:T(128)}, bf16[24,144,64]{1,2,0:T(8,128)(2,1)S(1)}, f32[24,144]{1,0:T(8,128)}, s32[24]{0:T(128)S(1)}, bf16[144,1536]{1,0:T(8,128)(2,1)S(1)}, ...) while((s32[]{:T(128)}, ...), condition=%wide.region_12.13_spmd.clone, body=%wide.region_9.12_spmd.clone.sunk | while | flops 104799600 | bytes 6301395 | solution.py:193
  1295.6 14.2 fusion.47
  1367.5 332.8 %while.29 = (s32[]{:T(128)}, bf16[24,144,64]{1,2,0:T(8,128)(2,1)S(1)}, f32[24,2736,64]{1,2,0:T(8,128)}, f32[24,2736,64]{1,2,0:T(8,128)}, s32[24]{0:T(128)S(1)}, ...) while((s32[]{:T(128)}, ...), condition=%wide.region_19.20_spmd.clone, body=%wide.region_17.19_spmd.clone.sunk | while | flops 256667760 | bytes 15618069 | solution.py:253
  1735.5 18.4 collective-permute-done.55
  1766.5 19.9 collective-permute-done.57
  1796.6 20.7 collective-permute-start.65
  1870.7 13.4 fusion.206
  1926.5 28.2 fusion.139
  1991.6 17.8 collective-permute-start.46
  2065.9 20.6 fusion.143
  2086.5 97.4 %pad_maximum_fusion = f32[3072,12288]{1,0:T(8,128)} fusion(f32[3072,4608]{1,0:T(8,128)} %fusion.143, f32[3072,6144]{1,0:T(8,128)} %fusion.139, f32[3072,1536]{1,0:T(8,128)} %fusion.135), kind=kLoop, calls=%fused_computation.61 | loop fusion | flops 75497472 | bytes 301989888 | tf_op jit(solution)/shard_map/concatenate | solution.py:282
  2186.8 29.0 fusion.86
  2252.2 105.8 %all-reduce.2 = bf16[4,2,9216]{2,0,1:T(4,128)(2,1)S(1)} all-reduce(f32[4,2,9216]{2,0,1:T(4,128)S(1)} %copy.187), channel_id=1, replica_groups=mesh['dev'=32] {'dev'}, use_global_device_ids=true, to_apply=%region_22.23 | all-reduce | flops 73728 | bytes 442368 | tf_op jit(solution)/shard_map/psum | solution.py:309
  2358.5 39.6 all-gather
  2401.4 1089.0 %reduce-scatter.3.cloned.1.call-done = f32[96,12288]{1,0:T(8,128)} async-done(((f32[3072,12288]{1,0:T(8,128)}), f32[96,12288]{1,0:T(8,128)}) %reduce-scatter.3.cloned.1.call-update) | async-done | bytes 4718608 | tf_op jit(solution)/shard_map/reduce_scatter | solution.py:281
  3498.3 652.2 %reduce-scatter.5.cloned.1.call-done = f32[384,1536]{1,0:T(8,128)} async-done(((f32[12288,1536]{1,0:T(8,128)}), f32[384,1536]{1,0:T(8,128)}) %reduce-scatter.5.cloned.1.call-update) | async-done | bytes 2359312 | tf_op jit(solution)/shard_map/reduce_scatter | solution.py:210
  (816 shorter events, 1023.4 us)
Async XLA Ops:
  7.2 311.4 %all-gather.7.cloned.1.call-start = ((), (), s32[]{:S(2)}) async-start(), calls=%async_computation.2 | async-start | bytes 58392576 | tf_op jit(solution)/shard_map/all_gather | solution.py:143
  7.9 480.9 %all-gather.9.cloned.1.call-start = ((), (), s32[]{:S(2)}) async-start(), calls=%async_computation.3 | async-start | bytes 29196288 | tf_op jit(solution)/shard_map/all_gather | solution.py:144
  8.7 1217.6 %all-gather.11.cloned.1.call-start = ((), (), s32[]{:S(2)}) async-start(), calls=%async_computation.4 | async-start | bytes 9732096 | tf_op jit(solution)/shard_map/all_gather | solution.py:81
  9.4 1233.9 %all-gather.13.cloned.1.call-start = ((), (), s32[]{:S(2)}) async-start(), calls=%async_computation.5 | async-start | bytes 38928384 | tf_op jit(solution)/shard_map/all_gather | solution.py:82
  10.0 1244.9 %all-gather.15.cloned.1.call-start = ((), (), s32[]{:S(2)}) async-start(), calls=%async_computation.6 | async-start | bytes 38928384 | tf_op jit(solution)/shard_map/all_gather | solution.py:83
  10.6 3479.8 %reduce-scatter.3.cloned.1.call-start = ((), (), s32[]{:S(2)}) async-start(), calls=%async_computation.7 | async-start | bytes 155713536 | tf_op jit(solution)/shard_map/reduce_scatter | solution.py:281
  514.6 380.2 %collective-permute-start.35 = (bf16[144,1536]{1,0:T(8,128)(2,1)S(1)}, bf16[144,1536]{1,0:T(8,128)(2,1)S(1)}, u32[]{:S(2)}, u32[]{:S(2)}) collective-permute-start(bf16[144,1536]{1,0:T(8,128)(2,1)S(1)} %get-tuple-element.282), channel_id=1, source_target_pairs={{9,0},{10,1},{11,2},{12,3},{13,4},{14,5},{15,6},{16,7},{17,8},{18,... | collective-permute-start | bytes 1327112 | tf_op jit(solution)/shard_map/ppermute | solution.py:22
  515.9 377.6 %collective-permute-start.34 = (bf16[144,1536]{1,0:T(8,128)(2,1)S(1)}, bf16[144,1536]{1,0:T(8,128)(2,1)S(1)}, u32[]{:S(2)}, u32[]{:S(2)}) collective-permute-start(bf16[144,1536]{1,0:T(8,128)(2,1)S(1)} %get-tuple-element.282), channel_id=1, source_target_pairs={{8,0},{9,1},{10,2},{11,3},{12,4},{13,5},{14,6},{15,7},{16,8},{17,9... | collective-permute-start | bytes 1327112 | tf_op jit(solution)/shard_map/ppermute | solution.py:22
  517.2 374.9 %collective-permute-start.33 = (bf16[144,1536]{1,0:T(8,128)(2,1)S(1)}, bf16[144,1536]{1,0:T(8,128)(2,1)S(1)}, u32[]{:S(2)}, u32[]{:S(2)}) collective-permute-start(bf16[144,1536]{1,0:T(8,128)(2,1)S(1)} %get-tuple-element.282), channel_id=1, source_target_pairs={{7,0},{8,1},{9,2},{10,3},{11,4},{12,5},{13,6},{14,7},{15,8},{16,9}... | collective-permute-start | bytes 1327112 | tf_op jit(solution)/shard_map/ppermute | solution.py:22
  770.6 76.0 %collective-permute-start.29 = (bf16[144,1536]{1,0:T(8,128)(2,1)S(1)}, bf16[144,1536]{1,0:T(8,128)(2,1)S(1)}, u32[]{:S(2)}, u32[]{:S(2)}) collective-permute-start(bf16[144,1536]{1,0:T(8,128)(2,1)S(1)} %get-tuple-element.282), channel_id=1, source_target_pairs={{3,0},{4,1},{5,2},{6,3},{7,4},{8,5},{9,6},{10,7},{11,8},{12,9},{13... | collective-permute-start | bytes 1327112 | tf_op jit(solution)/shard_map/ppermute | solution.py:22
  774.9 80.4 %collective-permute-start.30 = (bf16[144,1536]{1,0:T(8,128)(2,1)S(1)}, bf16[144,1536]{1,0:T(8,128)(2,1)S(1)}, u32[]{:S(2)}, u32[]{:S(2)}) collective-permute-start(bf16[144,1536]{1,0:T(8,128)(2,1)S(1)} %get-tuple-element.282), channel_id=1, source_target_pairs={{4,0},{5,1},{6,2},{7,3},{8,4},{9,5},{10,6},{11,7},{12,8},{13,9},{1... | collective-permute-start | bytes 1327112 | tf_op jit(solution)/shard_map/ppermute | solution.py:22
  889.5 167.2 %collective-permute-start.17 = (bf16[144,1536]{1,0:T(8,128)(2,1)S(1)}, bf16[144,1536]{1,0:T(8,128)(2,1)S(1)}, u32[]{:S(2)}, u32[]{:S(2)}) collective-permute-start(bf16[144,1536]{1,0:T(8,128)(2,1)S(1)} %get-tuple-element.283), channel_id=1, source_target_pairs={{9,0},{10,1},{11,2},{12,3},{13,4},{14,5},{15,6},{16,7},{17,8},{18,... | collective-permute-start | bytes 1327112 | tf_op jit(solution)/shard_map/ppermute | solution.py:22
  890.8 165.8 %collective-permute-start.16 = (bf16[144,1536]{1,0:T(8,128)(2,1)S(1)}, bf16[144,1536]{1,0:T(8,128)(2,1)S(1)}, u32[]{:S(2)}, u32[]{:S(2)}) collective-permute-start(bf16[144,1536]{1,0:T(8,128)(2,1)S(1)} %get-tuple-element.283), channel_id=1, source_target_pairs={{8,0},{9,1},{10,2},{11,3},{12,4},{13,5},{14,6},{15,7},{16,8},{17,9... | collective-permute-start | bytes 1327112 | tf_op jit(solution)/shard_map/ppermute | solution.py:22
  892.2 164.4 %collective-permute-start.15 = (bf16[144,1536]{1,0:T(8,128)(2,1)S(1)}, bf16[144,1536]{1,0:T(8,128)(2,1)S(1)}, u32[]{:S(2)}, u32[]{:S(2)}) collective-permute-start(bf16[144,1536]{1,0:T(8,128)(2,1)S(1)} %get-tuple-element.283), channel_id=1, source_target_pairs={{7,0},{8,1},{9,2},{10,3},{11,4},{12,5},{13,6},{14,7},{15,8},{16,9}... | collective-permute-start | bytes 1327112 | tf_op jit(solution)/shard_map/ppermute | solution.py:22
  894.9 73.6 %collective-permute-start.10 = (bf16[144,1536]{1,0:T(8,128)(2,1)S(1)}, bf16[144,1536]{1,0:T(8,128)(2,1)S(1)}, u32[]{:S(2)}, u32[]{:S(2)}) collective-permute-start(bf16[144,1536]{1,0:T(8,128)(2,1)S(1)} %get-tuple-element.283), channel_id=1, source_target_pairs={{2,0},{3,1},{4,2},{5,3},{6,4},{7,5},{8,6},{9,7},{10,8},{11,9},{12,... | collective-permute-start | bytes 1327112 | tf_op jit(solution)/shard_map/ppermute | solution.py:22
  897.2 75.4 %collective-permute-start.11 = (bf16[144,1536]{1,0:T(8,128)(2,1)S(1)}, bf16[144,1536]{1,0:T(8,128)(2,1)S(1)}, u32[]{:S(2)}, u32[]{:S(2)}) collective-permute-start(bf16[144,1536]{1,0:T(8,128)(2,1)S(1)} %get-tuple-element.283), channel_id=1, source_target_pairs={{3,0},{4,1},{5,2},{6,3},{7,4},{8,5},{9,6},{10,7},{11,8},{12,9},{13... | collective-permute-start | bytes 1327112 | tf_op jit(solution)/shard_map/ppermute | solution.py:22
  972.6 65.3 %collective-permute-start.13 = (bf16[144,1536]{1,0:T(8,128)(2,1)S(1)}, bf16[144,1536]{1,0:T(8,128)(2,1)S(1)}, u32[]{:S(2)}, u32[]{:S(2)}) collective-permute-start(bf16[144,1536]{1,0:T(8,128)(2,1)S(1)} %get-tuple-element.283), channel_id=1, source_target_pairs={{5,0},{6,1},{7,2},{8,3},{9,4},{10,5},{11,6},{12,7},{13,8},{14,9},{... | collective-permute-start | bytes 1327112 | tf_op jit(solution)/shard_map/ppermute | solution.py:22
  978.6 77.9 %collective-permute-start.14 = (bf16[144,1536]{1,0:T(8,128)(2,1)S(1)}, bf16[144,1536]{1,0:T(8,128)(2,1)S(1)}, u32[]{:S(2)}, u32[]{:S(2)}) collective-permute-start(bf16[144,1536]{1,0:T(8,128)(2,1)S(1)} %get-tuple-element.283), channel_id=1, source_target_pairs={{6,0},{7,1},{8,2},{9,3},{10,4},{11,5},{12,6},{13,7},{14,8},{15,9},... | collective-permute-start | bytes 1327112 | tf_op jit(solution)/shard_map/ppermute | solution.py:22
  1729.5 56.9 %collective-permute-start.57 = (bf16[144,1536]{1,0:T(8,128)(2,1)}, bf16[144,1536]{1,0:T(8,128)(2,1)}, u32[]{:S(2)}, u32[]{:S(2)}) collective-permute-start(bf16[144,1536]{1,0:T(8,128)(2,1)} %copy.216), channel_id=1, source_target_pairs={{6,0},{7,1},{8,2},{9,3},{10,4},{11,5},{12,6},{13,7},{14,8},{15,9},... | collective-permute-start | bytes 1327112 | tf_op jit(solution)/shard_map/ppermute | solution.py:22
  1734.2 59.3 %collective-permute-start.59 = (bf16[144,1536]{1,0:T(8,128)(2,1)}, bf16[144,1536]{1,0:T(8,128)(2,1)}, u32[]{:S(2)}, u32[]{:S(2)}) collective-permute-start(bf16[144,1536]{1,0:T(8,128)(2,1)} %copy.218), channel_id=1, source_target_pairs={{4,0},{5,1},{6,2},{7,3},{8,4},{9,5},{10,6},{11,7},{12,8},{13,9},{1... | collective-permute-start | bytes 1327112 | tf_op jit(solution)/shard_map/ppermute | solution.py:22
  1765.2 75.2 %collective-permute-start.61 = (bf16[144,1536]{1,0:T(8,128)(2,1)}, bf16[144,1536]{1,0:T(8,128)(2,1)}, u32[]{:S(2)}, u32[]{:S(2)}) collective-permute-start(bf16[144,1536]{1,0:T(8,128)(2,1)} %copy.220), channel_id=1, source_target_pairs={{2,0},{3,1},{4,2},{5,3},{6,4},{7,5},{8,6},{9,7},{10,8},{11,9},{12,... | collective-permute-start | bytes 1327112 | tf_op jit(solution)/shard_map/ppermute | solution.py:22
  1786.3 60.9 %collective-permute-start.62 = (bf16[144,1536]{1,0:T(8,128)(2,1)}, bf16[144,1536]{1,0:T(8,128)(2,1)}, u32[]{:S(2)}, u32[]{:S(2)}) collective-permute-start(bf16[144,1536]{1,0:T(8,128)(2,1)} %copy.221), channel_id=1, source_target_pairs={{1,0},{2,1},{3,2},{4,3},{5,4},{6,5},{7,6},{8,7},{9,8},{10,9},{11,1... | collective-permute-start | bytes 1327112 | tf_op jit(solution)/shard_map/ppermute | solution.py:22
  1787.6 64.6 %collective-permute-start.63 = (bf16[144,1536]{1,0:T(8,128)(2,1)}, bf16[144,1536]{1,0:T(8,128)(2,1)}, u32[]{:S(2)}, u32[]{:S(2)}) collective-permute-start(bf16[144,1536]{1,0:T(8,128)(2,1)} %copy.222), channel_id=1, source_target_pairs={{0,1},{1,2},{2,3},{3,4},{4,5},{5,6},{6,7},{7,8},{8,9},{9,10},{10,1... | collective-permute-start | bytes 1327112 | tf_op jit(solution)/shard_map/ppermute | solution.py:22
  1793.6 71.1 %collective-permute-start.64 = (bf16[144,1536]{1,0:T(8,128)(2,1)}, bf16[144,1536]{1,0:T(8,128)(2,1)}, u32[]{:S(2)}, u32[]{:S(2)}) collective-permute-start(bf16[144,1536]{1,0:T(8,128)(2,1)} %copy.223), channel_id=1, source_target_pairs={{0,2},{1,3},{2,4},{3,5},{4,6},{5,7},{6,8},{7,9},{8,10},{9,11},{10,... | collective-permute-start | bytes 1327112 | tf_op jit(solution)/shard_map/ppermute | solution.py:22
  1796.6 72.0 %collective-permute-start.65 = (bf16[144,1536]{1,0:T(8,128)(2,1)S(1)}, bf16[144,1536]{1,0:T(8,128)(2,1)}, u32[]{:S(2)}, u32[]{:S(2)}) collective-permute-start(bf16[144,1536]{1,0:T(8,128)(2,1)S(1)} %copy.224), channel_id=1, source_target_pairs={{0,3},{1,4},{2,5},{3,6},{4,7},{5,8},{6,9},{7,10},{8,11},{9,12},{10... | collective-permute-start | bytes 1327112 | tf_op jit(solution)/shard_map/ppermute | solution.py:22
  1840.4 59.9 %collective-permute-start.66 = (bf16[144,1536]{1,0:T(8,128)(2,1)}, bf16[144,1536]{1,0:T(8,128)(2,1)}, u32[]{:S(2)}, u32[]{:S(2)}) collective-permute-start(bf16[144,1536]{1,0:T(8,128)(2,1)} %copy.225), channel_id=1, source_target_pairs={{0,4},{1,5},{2,6},{3,7},{4,8},{5,9},{6,10},{7,11},{8,12},{9,13},{1... | collective-permute-start | bytes 1327112 | tf_op jit(solution)/shard_map/ppermute | solution.py:22
  1911.0 69.6 %collective-permute-start.40 = (bf16[144,1536]{1,0:T(8,128)(2,1)}, bf16[144,1536]{1,0:T(8,128)(2,1)}, u32[]{:S(2)}, u32[]{:S(2)}) collective-permute-start(bf16[144,1536]{1,0:T(8,128)(2,1)} %copy.198), channel_id=1, source_target_pairs={{5,0},{6,1},{7,2},{8,3},{9,4},{10,5},{11,6},{12,7},{13,8},{14,9},{... | collective-permute-start | bytes 1327112 | tf_op jit(solution)/shard_map/ppermute | solution.py:22
  1917.8 73.8 %collective-permute-start.41 = (bf16[144,1536]{1,0:T(8,128)(2,1)}, bf16[144,1536]{1,0:T(8,128)(2,1)}, u32[]{:S(2)}, u32[]{:S(2)}) collective-permute-start(bf16[144,1536]{1,0:T(8,128)(2,1)} %copy.199), channel_id=1, source_target_pairs={{4,0},{5,1},{6,2},{7,3},{8,4},{9,5},{10,6},{11,7},{12,8},{13,9},{1... | collective-permute-start | bytes 1327112 | tf_op jit(solution)/shard_map/ppermute | solution.py:22
  1922.5 86.9 %collective-permute-start.42 = (bf16[144,1536]{1,0:T(8,128)(2,1)}, bf16[144,1536]{1,0:T(8,128)(2,1)}, u32[]{:S(2)}, u32[]{:S(2)}) collective-permute-start(bf16[144,1536]{1,0:T(8,128)(2,1)} %copy.200), channel_id=1, source_target_pairs={{3,0},{4,1},{5,2},{6,3},{7,4},{8,5},{9,6},{10,7},{11,8},{12,9},{13... | collective-permute-start | bytes 1327112 | tf_op jit(solution)/shard_map/ppermute | solution.py:22
  1923.8 89.8 %collective-permute-start.43 = (bf16[144,1536]{1,0:T(8,128)(2,1)}, bf16[144,1536]{1,0:T(8,128)(2,1)}, u32[]{:S(2)}, u32[]{:S(2)}) collective-permute-start(bf16[144,1536]{1,0:T(8,128)(2,1)} %copy.201), channel_id=1, source_target_pairs={{2,0},{3,1},{4,2},{5,3},{6,4},{7,5},{8,6},{9,7},{10,8},{11,9},{12,... | collective-permute-start | bytes 1327112 | tf_op jit(solution)/shard_map/ppermute | solution.py:22
  1925.1 92.4 %collective-permute-start.44 = (bf16[144,1536]{1,0:T(8,128)(2,1)}, bf16[144,1536]{1,0:T(8,128)(2,1)}, u32[]{:S(2)}, u32[]{:S(2)}) collective-permute-start(bf16[144,1536]{1,0:T(8,128)(2,1)} %copy.202), channel_id=1, source_target_pairs={{1,0},{2,1},{3,2},{4,3},{5,4},{6,5},{7,6},{8,7},{9,8},{10,9},{11,1... | collective-permute-start | bytes 1327112 | tf_op jit(solution)/shard_map/ppermute | solution.py:22
  2183.9 1966.6 %reduce-scatter.5.cloned.1.call-start = ((), (), s32[]{:S(2)}) async-start(), calls=%async_computation.8 | async-start | bytes 77856768 | tf_op jit(solution)/shard_map/reduce_scatter | solution.py:210
  (123 other events, 8546.1 us)
Sparse Core Ops, SparseCore 0:
  10.9 307.6 all-gather.6
  321.5 167.2 all-gather.8
  491.7 104.8 all-gather.10
  599.4 330.0 all-gather.12
  932.3 274.2 all-gather.14
  2184.1 1306.2 reduce-scatter.2
  3497.4 653.0 reduce-scatter.4
where the time goes:
time: 4180 us; the launch traced here: 4160 us
  waiting for transfers between devices  2580 us (62%)
  matrix products  586 us (14%)
  starting transfers between devices  358 us (9%)
  local copies, waits for them, and re-layouts  237 us (6%)
  other arithmetic  152 us (4%)
  blocking collectives  145 us (3%)
  loops' own time  78.1 us (2%)
    reduce_scatter x1, waiting for transfers between devices, on_device(): lax.psum_scatter(jnp.concatenate([term_rows(attended_split, grad_merged),...  1090 us
    reduce_scatter x1, waiting for transfers between devices, on_device(): lax.psum_scatter(term_rows(activated_split, grad_lowered), 'dev', scatter...  652 us
    ppermute x72, waiting for transfers between devices, passed_along(): return lax.ppermute(x, axis, pairs)  391 us
    ppermute x72, starting transfers between devices, passed_along(): return lax.ppermute(x, axis, pairs)  358 us
    all_gather x1, waiting for transfers between devices, on_device(): lax.all_gather(modulation_weight, 'dev', axis=0, tiled=True)  306 us
    all_gather x1, waiting for transfers between devices, on_device(): lax.all_gather(project_weight, 'dev', axis=0, tiled=True)  142 us
    psum x1, blocking collectives, on_device(): lax.psum(local_table.reshape(seq_count, 2, 6 * width), 'dev')  106 us
    concatenate x1, other arithmetic, on_device(): jnp.concatenate([term_rows(attended_split, grad_merged), term_rows(hidden...  97.4 us
  transfers between devices with their start and end apart: 79, of which 30 were waited for; matrix products, arithmetic and copies ran while one was open for 11% of the time, Pallas kernels for 0%

commit v1 on v0

v1 whole, which is shorter than its diff:
```python
import jax
import jax.numpy as jnp
from jax import lax
from jax.experimental import pallas as pl
from jax.experimental.pallas import tpu as pltpu
from jax.sharding import Mesh
from jax.sharding import PartitionSpec as P

HEADS = 24
HDIM = 64
IMG = 1024
RANKS = 8
TXT_PAD = 256
SEQ = IMG + TXT_PAD
IMG_ROWS = IMG // RANKS
TXT_ROWS = TXT_PAD // RANKS
CHUNK = IMG_ROWS + TXT_ROWS
RANK_HEADS = HEADS // RANKS
HEAD_COLS = RANK_HEADS * HDIM
Q_BLOCK = 256
EPSILON = 1e-06
CONTRACT_LAST = (((1,), (1,)), ((), ()))
CONTRACT_FIRST = (((0,), (0,)), ((), ()))
CORES = 2
ALL = ("h", "u", "p", "c")
HALF = ("u", "p", "c")
PLANES = ("h", "u")
RANK = ("p", "c")
HALF_CHIPS = ("u", "p")
LINE = 4
BF = jnp.bfloat16
F32 = jnp.float32


def dot(a, b):
    return jnp.dot(a, b, preferred_element_type=F32)


def dot_last(a, b):
    return lax.dot_general(a, b, CONTRACT_LAST, preferred_element_type=F32)


def dot_first(a, b):
    return lax.dot_general(a, b, CONTRACT_FIRST, preferred_element_type=F32)


def swap(x, axes):
    return lax.all_to_all(x, axes, 0, 0, tiled=True)


def to_all(x, axes):
    count = 1
    for axis in axes:
        count *= lax.axis_size(axis)
    return swap(jnp.broadcast_to(x[None], (count,) + x.shape), axes)


def layer_norm(values):
    mean = jnp.mean(values, axis=-1, keepdims=True)
    centred = values - mean
    variance = jnp.mean(centred * centred, axis=-1, keepdims=True)
    inv_std = lax.rsqrt(variance + EPSILON)
    return (centred * inv_std, inv_std)


def norm_back(grad_normed, normed, inv_std):
    mean_grad = jnp.mean(grad_normed, axis=-1, keepdims=True)
    mean_cross = jnp.mean(grad_normed * normed, axis=-1, keepdims=True)
    return inv_std * (grad_normed - mean_grad - normed * mean_cross)


def attention_forward_body(length_ref, qkv_ref, out_ref, log_ref):
    rows = pl.ds(pl.multiple_of(pl.program_id(0) * Q_BLOCK, Q_BLOCK), Q_BLOCK)
    key_ok = lax.broadcasted_iota(jnp.int32, (Q_BLOCK, SEQ), 1) < length_ref[0]
    for head in range(RANK_HEADS):
        cols = slice(head * HDIM, (head + 1) * HDIM)
        key_cols = slice(HEAD_COLS + head * HDIM, HEAD_COLS + (head + 1) * HDIM)
        value_cols = slice(2 * HEAD_COLS + head * HDIM, 2 * HEAD_COLS + (head + 1) * HDIM)
        query = qkv_ref[rows, cols] * BF(HDIM ** (-0.5))
        scores = jnp.where(key_ok, dot_last(query, qkv_ref[:, key_cols]), -1e30)
        top = jnp.max(scores, axis=1, keepdims=True)
        exponent = jnp.exp(scores - top)
        total = jnp.sum(exponent, axis=1, keepdims=True)
        probs = (exponent * (1.0 / total)).astype(BF)
        out_ref[:, cols] = dot(probs, qkv_ref[:, value_cols]).astype(BF)
        log_ref[:, head : head + 1] = top + jnp.log(total)


def attention_forward(length, qkv):
    return pl.pallas_call(
        attention_forward_body,
        grid=(SEQ // Q_BLOCK,),
        in_specs=[
            pl.BlockSpec(memory_space=pltpu.SMEM),
            pl.BlockSpec((SEQ, 3 * HEAD_COLS), lambda i: (0, 0)),
        ],
        out_specs=[
            pl.BlockSpec((Q_BLOCK, HEAD_COLS), lambda i: (i, 0)),
            pl.BlockSpec((Q_BLOCK, RANK_HEADS), lambda i: (i, 0)),
        ],
        out_shape=[
            jax.ShapeDtypeStruct((SEQ, HEAD_COLS), BF),
            jax.ShapeDtypeStruct((SEQ, RANK_HEADS), F32),
        ],
        cost_estimate=pl.CostEstimate(
            flops=4 * SEQ * SEQ * HEAD_COLS,
            bytes_accessed=8 * SEQ * HEAD_COLS,
            transcendentals=SEQ * SEQ * RANK_HEADS,
        ),
        name="attention_forward",
    )(length, qkv)


def attention_backward_body(length_ref, qkv_ref, grad_ref, log_ref, out_ref, sums):
    step = pl.program_id(0)
    rows = pl.ds(pl.multiple_of(step * Q_BLOCK, Q_BLOCK), Q_BLOCK)
    scale = HDIM ** (-0.5)

    @pl.when(step == 0)
    def _():
        sums[...] = jnp.zeros_like(sums)

    key_ok = lax.broadcasted_iota(jnp.int32, (Q_BLOCK, SEQ), 1) < length_ref[0]
    for head in range(RANK_HEADS):
        cols = slice(head * HDIM, (head + 1) * HDIM)
        next_cols = slice(HEAD_COLS + head * HDIM, HEAD_COLS + (head + 1) * HDIM)
        last_cols = slice(2 * HEAD_COLS + head * HDIM, 2 * HEAD_COLS + (head + 1) * HDIM)
        query = qkv_ref[rows, cols] * BF(scale)
        keys = qkv_ref[:, next_cols]
        grad = grad_ref[:, cols]
        scores = dot_last(query, keys)
        probs = jnp.where(key_ok, jnp.exp(scores - log_ref[:, head : head + 1]), 0.0)
        grad_probs = dot_last(grad, qkv_ref[:, last_cols])
        inner = jnp.sum(probs * grad_probs, axis=1, keepdims=True)
        grad_scores = (probs * (grad_probs - inner)).astype(BF)
        out_ref[rows, cols] = (dot(grad_scores, keys) * scale).astype(BF)
        sums[:, cols] += dot_first(grad_scores, query)
        sums[:, next_cols] += dot_first(probs.astype(BF), grad)

    @pl.when(step == pl.num_programs(0) - 1)
    def _():
        out_ref[:, HEAD_COLS:] = sums[...].astype(BF)


def attention_backward(length, qkv, grad, logs):
    return pl.pallas_call(
        attention_backward_body,
        grid=(SEQ // Q_BLOCK,),
        in_specs=[
            pl.BlockSpec(memory_space=pltpu.SMEM),
            pl.BlockSpec((SEQ, 3 * HEAD_COLS), lambda i: (0, 0)),
            pl.BlockSpec((Q_BLOCK, HEAD_COLS), lambda i: (i, 0)),
            pl.BlockSpec((Q_BLOCK, RANK_HEADS), lambda i: (i, 0)),
        ],
        out_specs=pl.BlockSpec((SEQ, 3 * HEAD_COLS), lambda i: (0, 0)),
        out_shape=jax.ShapeDtypeStruct((SEQ, 3 * HEAD_COLS), BF),
        scratch_shapes=[pltpu.VMEM((SEQ, 2 * HEAD_COLS), F32)],
        cost_estimate=pl.CostEstimate(
            flops=10 * SEQ * SEQ * HEAD_COLS,
            bytes_accessed=14 * SEQ * HEAD_COLS,
            transcendentals=SEQ * SEQ * RANK_HEADS,
        ),
        name="attention_backward",
    )(length, qkv, grad, logs)


def split_halves(first, image, text):
    return jnp.where(first, text, image).astype(BF), jnp.where(first, image, text)


def own_rows(sequence, rank):
    return jnp.concatenate(
        [
            lax.dynamic_slice_in_dim(sequence, rank * IMG_ROWS, IMG_ROWS, 0),
            lax.dynamic_slice_in_dim(sequence, IMG + rank * TXT_ROWS, TXT_ROWS, 0),
        ],
        axis=0,
    )


def by_stream(chunks):
    width = chunks.shape[-1]
    chunks = chunks.reshape(-1, CHUNK, width)
    return (
        chunks[:, :IMG_ROWS].reshape(-1, width),
        chunks[:, IMG_ROWS:].reshape(-1, width),
    )


def to_chunks(image, text):
    width = image.shape[-1]
    return jnp.concatenate(
        [image.reshape(-1, IMG_ROWS, width), text.reshape(-1, TXT_ROWS, width)], axis=1
    )


def pair_blocks(blocks):
    pairs = blocks.reshape((-1, CORES) + blocks.shape[1:])
    first = lax.axis_index("c") == 0
    keep = jnp.where(first, pairs[:, 0], pairs[:, 1])
    send = jnp.where(first, pairs[:, 1], pairs[:, 0])
    got = lax.ppermute(send, "c", [(0, 1), (1, 0)])
    return (keep.astype(F32) + got.astype(F32)).astype(BF)


def total(parts):
    return jnp.sum(parts.astype(F32), axis=0)


def next_planes(rising, falling, planes):
    return (
        lax.ppermute(rising, PLANES, step_planes(1, planes)),
        lax.ppermute(falling, PLANES, step_planes(-1, planes)),
    )


def exchange_planes(parts, planes, plane):
    got = []
    for by in range(1, planes):
        send = lax.dynamic_index_in_dim(parts, (plane + by) % planes, 0, keepdims=False)
        got.append(lax.ppermute(send, PLANES, [(i, (i + by) % planes) for i in range(planes)]))
    return got


def sum_planes(parts, got, plane):
    result = lax.dynamic_index_in_dim(parts, plane, 0, keepdims=False).astype(F32)
    for piece in got:
        result = result + piece.astype(F32)
    return result


def place_rows(sequence, place, halo, count):
    zeros = jnp.zeros((2 * halo, sequence.shape[1]), sequence.dtype)
    padded = jnp.concatenate([zeros, sequence, zeros])
    return lax.dynamic_slice_in_dim(padded, 2 * halo - place, count + 2 * halo, 0)


def stream_rows(table, image_count, text_count):
    is_text = lax.broadcasted_iota(jnp.int32, (image_count + text_count, 1), 0) >= image_count
    return jnp.where(is_text, table[1][None, :], table[0][None, :])


def stream_sums(rows, image_count):
    return jnp.stack([jnp.sum(rows[:image_count], axis=0), jnp.sum(rows[image_count:], axis=0)])


def step_planes(by, planes):
    return [(i, i + by) for i in range(planes) if 0 <= i + by < planes]


def neighbour_rows(from_before, from_after, rank, rows_dev):
    halo, width = from_before.shape
    spans = -(-halo // rows_dev)
    pad = spans * rows_dev - halo
    zeros = jnp.zeros((rows_dev, width), from_before.dtype)
    front = jnp.concatenate([from_before, jnp.zeros((pad, width), from_before.dtype), zeros])
    back = jnp.concatenate([zeros, jnp.zeros((pad, width), from_after.dtype), from_after])
    from_end = RANKS - 1 - rank
    front_at = jnp.minimum(rank, spans) * rows_dev
    back_at = (spans - jnp.minimum(from_end, spans)) * rows_dev
    return lax.dynamic_slice_in_dim(front, front_at, rows_dev, 0) + lax.dynamic_slice_in_dim(
        back, back_at, rows_dev, 0
    )


def layer(
    tokens,
    conditioning,
    text_lengths,
    modulation_weight,
    project_weight,
    merge_weight,
    up_weight,
    down_weight,
    cotangent,
):
    rows_dev, width = tokens.shape
    shard = modulation_weight.shape[0]
    ff_rows = down_weight.shape[0]
    seqs = conditioning.shape[0]
    per_half = lax.axis_size("u")
    planes = 2 * per_half
    half_devices = per_half * RANKS
    devices = 2 * half_devices
    half = lax.axis_index("h")
    rank = lax.axis_index(RANK)
    plane = half * per_half + lax.axis_index("u")
    device = plane * RANKS + rank
    group_rows = RANKS * rows_dev
    halo = -(-13 * seqs // 16) * 16
    mod_cols = 6 * width // RANKS
    other_half = [(0, 1), (1, 0)]

    lengths = IMG + text_lengths
    starts = jnp.cumsum(lengths) - lengths
    length = lax.dynamic_index_in_dim(lengths, plane, 0, keepdims=False)
    start = lax.dynamic_index_in_dim(starts, plane, 0, keepdims=False)
    place = halo + start - plane * group_rows
    valid = (jnp.arange(SEQ, dtype=jnp.int32) < length)[:, None]
    length_arg = length.reshape(1)

    group = lax.all_gather(tokens, RANK, axis=0, tiled=True)
    before = lax.ppermute(group[-halo:], PLANES, step_planes(1, planes))
    after = lax.ppermute(group[:halo], PLANES, step_planes(-1, planes))
    extra = SEQ - group_rows
    window = jnp.concatenate([before, group, after, jnp.zeros((extra, width), BF)])
    sequence = lax.dynamic_slice_in_dim(window, place, SEQ, 0)
    sequence = jnp.where(valid, sequence, jnp.zeros_like(sequence))

    mine = project_weight.reshape(shard, 3, RANKS, HEAD_COLS).transpose(2, 0, 1, 3)
    mine = swap(mine.reshape(RANKS, shard, 3 * HEAD_COLS), RANK)
    mine = mine.reshape(RANKS * shard, 3 * HEAD_COLS)
    rising, falling = [mine], [mine]
    if planes <= LINE:
        up, down = next_planes(mine, mine, planes)
        rising.append(up)
        falling.append(down)

    cond_float = conditioning.astype(F32)
    silu_low = jax.nn.silu(cond_float).astype(BF)
    silu_part = lax.dynamic_slice_in_dim(silu_low, device * shard % width, shard, 1)
    mod_part = dot(silu_part, modulation_weight).reshape(devices, mod_cols)
    mod_mine = jnp.sum(swap(mod_part, ALL).reshape(2, half_devices, mod_cols), axis=1)
    mod_mine, rising, falling = lax.optimization_barrier((mod_mine, rising, falling))

    if planes <= LINE:
        up, down = next_planes(rising[-1], falling[-1], planes)
        rising.append(up)
        falling.append(down)

    mods_half = (
        to_all(mod_mine, HALF)
        .reshape(per_half, RANKS, 2, mod_cols)
        .transpose(0, 2, 1, 3)
        .reshape(per_half, 2, 6, width)
    )
    mods_half, rising, falling = lax.optimization_barrier((mods_half, rising, falling))
    mods = lax.dynamic_index_in_dim(mods_half, lax.axis_index("u"), 0, keepdims=False)
    shift_a, scale_a, gate_a, shift_b, scale_b, gate_b = [mods[:, i] for i in range(6)]

    if planes <= LINE:
        for _ in range(planes - 3):
            up, down = next_planes(rising[-1], falling[-1], planes)
            rising.append(up)
            falling.append(down)
        pieces = jnp.stack(rising[:0:-1] + falling)
        project = lax.dynamic_slice_in_dim(pieces, planes - 1 - plane, planes, 0)
    else:
        project = lax.all_gather(mine, PLANES, axis=0, tiled=True)
    project = project.reshape(2 * width, 3 * HEAD_COLS)

    normed_a, inv_a = layer_norm(sequence.astype(F32))
    hidden_a = (
        normed_a * (1.0 + stream_rows(scale_a, IMG, TXT_PAD)) + stream_rows(shift_a, IMG, TXT_PAD)
    ).astype(BF)

    up_own = swap(up_weight.reshape(shard, half_devices, ff_rows).transpose(1, 0, 2), HALF)
    up_own = up_own.reshape(width, ff_rows)
    project, up_own, down_own, hidden_a = lax.optimization_barrier(
        (project, up_own, down_weight, hidden_a)
    )
    project_image, project_text = project[:width], project[width:]
    merge = lax.all_gather(merge_weight, ALL, axis=0, tiled=True)
    merge_image, merge_text = merge[:width], merge[width:]
    up_other = lax.ppermute(up_own, "h", other_half)
    down_other = lax.ppermute(down_own, "h", other_half)
    first = half == 0
    up_image = jnp.where(first, up_own, up_other)
    up_text = jnp.where(first, up_other, up_own)
    down_image = jnp.where(first, down_own, down_other)
    down_text = jnp.where(first, down_other, down_own)

    cot_half = lax.all_gather(cotangent, HALF, axis=0, tiled=True)
    edge = jnp.where(first, cot_half[-halo:], cot_half[:halo])
    edge = lax.ppermute(edge, "h", other_half)
    none = jnp.zeros_like(edge)
    cot_window = jnp.concatenate(
        [
            jnp.where(first, none, edge),
            cot_half,
            jnp.where(first, edge, none),
            jnp.zeros((extra, width), BF),
        ]
    )
    cot_image, cot_text = [], []
    for index in range(per_half):
        seq = half * per_half + index
        at = halo + starts[seq] - half * per_half * group_rows
        text_ok = (jnp.arange(TXT_PAD, dtype=jnp.int32) < text_lengths[seq])[:, None]
        cot_image.append(lax.dynamic_slice_in_dim(cot_window, at, IMG, 0))
        text = lax.dynamic_slice_in_dim(cot_window, at + IMG, TXT_PAD, 0)
        cot_text.append(jnp.where(text_ok, text, jnp.zeros_like(text)))
    low_image = jnp.concatenate(
        [(mods_half[i, 0, 5][None] * cot_image[i].astype(F32)).astype(BF) for i in range(per_half)]
    )
    low_text = jnp.concatenate(
        [(mods_half[i, 1, 5][None] * cot_text[i].astype(F32)).astype(BF) for i in range(per_half)]
    )
    which = lax.axis_index("u")
    cot_rows = jnp.concatenate(
        [
            lax.dynamic_slice_in_dim(
                jnp.concatenate(cot_image), which * IMG + rank * IMG_ROWS, IMG_ROWS, 0
            ),
            lax.dynamic_slice_in_dim(
                jnp.concatenate(cot_text), which * TXT_PAD + rank * TXT_ROWS, TXT_ROWS, 0
            ),
        ]
    ).astype(F32)

    qkv = jnp.concatenate(
        [dot(hidden_a[:IMG], project_image), dot(hidden_a[IMG:], project_text)]
    ).astype(BF)

    attended, logs = attention_forward(length_arg, qkv)

    attended_rows = swap(to_chunks(attended[:IMG], attended[IMG:]), RANK)
    attended_rows = attended_rows.transpose(1, 0, 2).reshape(CHUNK, width)
    merged = jnp.concatenate(
        [dot(attended_rows[:IMG_ROWS], merge_image), dot(attended_rows[IMG_ROWS:], merge_text)]
    )
    token_rows = own_rows(sequence, rank).astype(F32)
    gate_a_rows = stream_rows(gate_a, IMG_ROWS, TXT_ROWS)
    scale_b_rows = 1.0 + stream_rows(scale_b, IMG_ROWS, TXT_ROWS)
    gate_b_rows = stream_rows(gate_b, IMG_ROWS, TXT_ROWS)
    middle = token_rows + gate_a_rows * merged
    normed_b, inv_b = layer_norm(middle)
    hidden_b = (normed_b * scale_b_rows + stream_rows(shift_b, IMG_ROWS, TXT_ROWS)).astype(BF)

    hidden_all = lax.all_gather(hidden_b, HALF, axis=0, tiled=True)
    att_cols = attended_rows.reshape(CHUNK, per_half, RANKS, shard).transpose(2, 0, 1, 3)
    att_cols = swap(att_cols.reshape(RANKS, CHUNK, per_half * shard), RANK)
    hidden_all, att_cols = lax.optimization_barrier((hidden_all, att_cols))
    hidden_image, hidden_text = by_stream(hidden_all)

    def feed(hidden, up, down, low):
        upper = dot(hidden, up)
        gelu, pull = jax.vjp(lambda value: jax.nn.gelu(value, approximate=True), upper)
        activated = gelu.astype(BF)
        lowered = dot(activated, down)
        grad_upper = pull(dot_last(low, down))[0].astype(BF)
        grad_hidden = dot_last(grad_upper, up)
        return activated, lowered, grad_upper, grad_hidden

    act_image, lowered_image, gu_image, gh_image = feed(
        hidden_image, up_image, down_image, low_image
    )
    act_text, lowered_text, gu_text, gh_text = feed(hidden_text, up_text, down_text, low_text)

    gh_pair = pair_blocks(to_chunks(gh_image.astype(BF), gh_text.astype(BF)))
    gh_parts = swap(gh_pair, HALF_CHIPS)
    low_pair = pair_blocks(to_chunks(lowered_image.astype(BF), lowered_text.astype(BF)))
    down_send, down_keep = split_halves(
        first, dot_first(act_image, low_image), dot_first(act_text, low_text)
    )
    up_send, up_keep = split_halves(
        first, dot_first(hidden_image, gu_image), dot_first(hidden_text, gu_text)
    )
    gh_parts, down_send, up_send, low_pair = lax.optimization_barrier(
        (gh_parts, down_send, up_send, low_pair)
    )
    grad_hidden_b = total(gh_parts)
    down_got = lax.ppermute(down_send, "h", other_half)
    up_got = lax.ppermute(up_send, "h", other_half)

    grad_scale_b = grad_hidden_b * normed_b
    grad_middle = cot_rows + norm_back(grad_hidden_b * scale_b_rows, normed_b, inv_b)
    grad_gate_a = grad_middle * merged
    grad_merged = (gate_a_rows * grad_middle).astype(BF)
    grad_attended = jnp.concatenate(
        [
            dot_last(grad_merged[:IMG_ROWS], merge_image),
            dot_last(grad_merged[IMG_ROWS:], merge_text),
        ]
    ).astype(BF)
    by_head = swap(grad_attended.reshape(CHUNK, RANKS, HEAD_COLS).transpose(1, 0, 2), RANK)
    by_head, low_pair, grad_merged = lax.optimization_barrier((by_head, low_pair, grad_merged))
    low_parts = swap(low_pair, HALF_CHIPS)
    gm_all = lax.all_gather(grad_merged, RANK, axis=0, tiled=True)
    grad_heads = jnp.concatenate(by_stream(by_head))

    grad_projected = attention_backward(length_arg, qkv, grad_heads, logs)

    part = jnp.concatenate(
        [
            dot_first(hidden_a[:IMG], grad_projected[:IMG]).astype(BF),
            dot_first(hidden_a[IMG:], grad_projected[IMG:]).astype(BF),
        ]
    )
    part = part.reshape(planes, RANKS * shard, 3 * HEAD_COLS)
    part, grad_projected = lax.optimization_barrier((part, grad_projected))
    part_got = exchange_planes(part, planes, plane)

    grad_hidden_a = jnp.concatenate(
        [
            dot_last(grad_projected[:IMG], project_image),
            dot_last(grad_projected[IMG:], project_text),
        ]
    )
    back = norm_back(grad_hidden_a * (1.0 + stream_rows(scale_a, IMG, TXT_PAD)), normed_a, inv_a)
    image_at, text_at = rank * IMG_ROWS, IMG + rank * TXT_ROWS
    mine = own_rows(back, rank) + grad_middle
    back = lax.dynamic_update_slice_in_dim(back, mine[:IMG_ROWS], image_at, 0)
    back = lax.dynamic_update_slice_in_dim(back, mine[IMG_ROWS:], text_at, 0)
    back_window = place_rows(back.astype(BF), place, halo, group_rows)
    ends = halo + group_rows
    blocks = jnp.concatenate(
        [
            back_window[halo:ends].reshape(RANKS, rows_dev, width),
            back_window[:halo].reshape(RANKS, halo // RANKS, width),
            back_window[ends : ends + halo].reshape(RANKS, halo // RANKS, width),
        ],
        axis=1,
    )
    back_pair = pair_blocks(blocks)
    back_pair, low_parts = lax.optimization_barrier((back_pair, low_parts))
    back_parts = swap(back_pair, ("p",))
    back_parts, gm_all, down_got, up_got, low_parts = lax.optimization_barrier(
        (back_parts, gm_all, down_got, up_got, low_parts)
    )
    summed = total(back_parts)
    edges = summed[rows_dev:].reshape(2, halo // RANKS, width)
    to_before = lax.ppermute(edges[0], PLANES, step_planes(-1, planes))
    to_after = lax.ppermute(edges[1], PLANES, step_planes(1, planes))
    to_before, to_after, part_got = lax.optimization_barrier((to_before, to_after, part_got))
    edges = to_all(jnp.stack([to_after, to_before]), RANK)
    edges = edges.reshape(RANKS, 2, halo // RANKS, width).transpose(1, 0, 2, 3)
    edges = edges.reshape(2, halo, width)
    tokens_grad = summed[:rows_dev] + neighbour_rows(edges[0], edges[1], rank, rows_dev)

    lowered = total(low_parts)
    layer_rows = (middle + gate_b_rows * lowered).astype(BF)
    layer_seq = jnp.concatenate(by_stream(lax.all_gather(layer_rows, RANK, axis=0, tiled=True)))
    layer_seq = jnp.where(valid, layer_seq, jnp.zeros_like(layer_seq))
    layer_window = place_rows(layer_seq, place, halo, group_rows)
    to_before = lax.ppermute(layer_window[:halo], PLANES, step_planes(-1, planes))
    to_after = lax.ppermute(
        layer_window[halo + group_rows : 2 * halo + group_rows], PLANES, step_planes(1, planes)
    )
    layer_out = lax.dynamic_slice_in_dim(
        layer_window, halo + rank * rows_dev, rows_dev, 0
    ) + neighbour_rows(to_after, to_before, rank, rows_dev)
    grad_gate_b = cot_rows * lowered

    down_grad = down_keep + down_got.astype(F32)
    up_cols = up_keep + up_got.astype(F32)
    up_grad = swap(up_cols.astype(BF).reshape(half_devices, shard, ff_rows), HALF)
    up_grad = up_grad.transpose(1, 0, 2).reshape(shard, half_devices * ff_rows).astype(F32)

    att_image, att_text = by_stream(att_cols)
    gm_image, gm_text = by_stream(gm_all)
    merge_part = jnp.stack([dot_first(att_image, gm_image), dot_first(att_text, gm_text)])
    merge_part = merge_part.astype(BF).reshape(planes, shard, width)
    merge_grad = sum_planes(merge_part, exchange_planes(merge_part, planes, plane), plane)

    part = sum_planes(part, part_got, plane).astype(BF)
    part = swap(part.reshape(RANKS, shard, 3 * HEAD_COLS), RANK)
    part = part.reshape(RANKS, shard, 3, HEAD_COLS).transpose(1, 2, 0, 3)
    project_grad = part.reshape(shard, 3 * width).astype(F32)

    grads = jnp.stack(
        [
            stream_sums(grad_hidden_a, IMG),
            stream_sums(grad_hidden_a * normed_a, IMG),
            stream_sums(grad_gate_a, IMG_ROWS),
            stream_sums(grad_hidden_b, IMG_ROWS),
            stream_sums(grad_scale_b, IMG_ROWS),
            stream_sums(grad_gate_b, IMG_ROWS),
        ],
        axis=1,
    )
    grads = grads.reshape(2, RANKS, mod_cols).transpose(1, 0, 2)
    grads = jnp.sum(swap(grads, RANK), axis=0).astype(BF)
    own_grads = swap(jnp.repeat(grads, half_devices, axis=0), ALL).reshape(seqs, 6 * width)
    modulation_grad = dot_first(silu_part, own_grads)
    piece = dot_last(own_grads, modulation_weight)
    pieces = to_all(piece, ALL).reshape(2, half_devices, seqs, shard)
    grad_silu = jnp.sum(pieces, axis=0).transpose(1, 0, 2).reshape(seqs, width)
    conditioning_grad = jax.vjp(jax.nn.silu, cond_float)[1](grad_silu)[0]

    return (
        layer_out,
        tokens_grad,
        conditioning_grad,
        modulation_grad,
        project_grad,
        merge_grad,
        up_grad,
        down_grad,
    )


def solution(mesh):
    count = mesh.devices.size
    grid = Mesh(mesh.devices.reshape(2, count // (2 * RANKS), RANKS // CORES, CORES), ALL)
    rows = P(ALL, None)
    return jax.shard_map(
        layer,
        mesh=grid,
        in_specs=(rows, P(), P(), rows, rows, rows, rows, rows, rows),
        out_specs=(rows, rows, P(), rows, rows, rows, rows, rows),
        check_vma=False,
    )
```

time: 4180 us -> 945 us (0.23)
  waiting for transfers between devices: 2580 us -> 367 us
  matrix products: 586 us -> 91.8 us
  starting transfers between devices: 358 us -> 123 us
  blocking collectives: 145 us -> 19.5 us
  local copies, waits for them, and re-layouts: 237 us -> 133 us
  loops' own time: 78.1 us -> 0 us
    reduce_scatter x2 -> x0, waiting for transfers between devices: 1740 us -> none  [the longest x1 1090 us: on_device(): lax.psum_scatter(jnp.concatenate([term_rows(attended_split, grad_merged),...]
    dot_general x193 -> x27, matrix products: 586 us -> 91.8 us  [the longest x9 36.9 us: dot_last(): return lax.dot_general(a, b, CONTRACT_LAST, preferred_element_type=F32)]
    all_gather x5 -> x6, waiting for transfers between devices: 448 us -> 41.8 us  [the longest x1 41.8 us: layer(): hidden_all = lax.all_gather(hidden_b, HALF, axis=0, tiled=True)]
    ppermute x72 -> x26, starting transfers between devices: 358 us -> 46.8 us  [the longest x3 14.8 us: next_planes(): lax.ppermute(rising, PLANES, step_planes(1, planes))]
    ppermute x72 -> x26, waiting for transfers between devices: 391 us -> 195 us  [the longest x1 78.3 us: layer(): down_got = lax.ppermute(down_send, 'h', other_half)]
    all_to_all x0 -> x15, waiting for transfers between devices: none -> 128 us  [swap(): return lax.all_to_all(x, axes, 0, 0, tiled=True)]
    psum x1 -> x0, blocking collectives: 106 us -> none  [on_device(): lax.psum(local_table.reshape(seq_count, 2, 6 * width), 'dev')]
    concatenate x4 -> x10, other arithmetic: 98.6 us -> 19.8 us  [the longest x2 5.3 us: place_rows(): padded = jnp.concatenate([zeros, sequence, zeros])]
  transfers between devices with their start and end apart: 79 -> 47, of which waited for: 30 -> 22; matrix products, arithmetic and copies ran while one was open for 11% -> 30% of each run, Pallas kernels for 0% -> 2%
where the time goes in v1:
time: 945 us; the launch traced here: 935 us
  waiting for transfers between devices  367 us (39%)
  other arithmetic  143 us (15%)
  local copies, waits for them, and re-layouts  133 us (14%)
  starting transfers between devices  123 us (13%)
  matrix products  91.8 us (10%)
  Pallas kernels  39.1 us (4%)
  blocking collectives  19.5 us (2%)
  between operations  18.3 us (2%)
    all_to_all x15, waiting for transfers between devices, swap(): return lax.all_to_all(x, axes, 0, 0, tiled=True)  128 us
    ppermute x1, waiting for transfers between devices, layer(): down_got = lax.ppermute(down_send, 'h', other_half)  78.3 us
    all_to_all x15, starting transfers between devices, swap(): return lax.all_to_all(x, axes, 0, 0, tiled=True)  76 us
    all_gather x1, waiting for transfers between devices, layer(): hidden_all = lax.all_gather(hidden_b, HALF, axis=0, tiled=True)  41.8 us
    dot_general x9, matrix products, dot_last(): return lax.dot_general(a, b, CONTRACT_LAST, preferred_element_type=F32)  36.9 us
    ppermute x3, waiting for transfers between devices, next_planes(): lax.ppermute(rising, PLANES, step_planes(1, planes))  36.3 us
    dot_general x9, matrix products, dot(): return jnp.dot(a, b, preferred_element_type=F32)  29 us
    dot_general x9, matrix products, dot_first(): return lax.dot_general(a, b, CONTRACT_FIRST, preferred_element_type=F32)  25.9 us
  transfers between devices with their start and end apart: 47, of which 22 were waited for; matrix products, arithmetic and copies ran while one was open for 30% of the time, Pallas kernels for 2%

profile of v1, /device:TPU:0, one launch (start us, length us, event | category | flops | bytes accessed | tf_op | source)
XLA Modules:
  0.0 934.9 jit_solution(11408129385823157306)
XLA Ops:
  14.9 5.3 all-to-all-start.1
  21.0 18.0 %all-to-all-done.1 = bf16[8,96,576]{2,1,0:T(8,128)(2,1)S(1)} async-done(((bf16[8,96,576]{2,1,0:T(8,128)(2,1)}), bf16[8,96,576]{2,1,0:T(8,128)(2,1)S(1)}, u32[]{:S(2)}, u32[]{:S(2)}) %all-to-all-start.1) | async-done | bytes 884768 | tf_op jit(solution)/shard_map/all_to_all | solution.py:48
  41.5 5.5 collective-permute-start.2
  48.3 19.5 %all_to_all.89 = f32[32,1,1152]{2,1,0:T(1,128)S(1)} all-to-all(f32[32,1,1152]{2,1,0:T(1,128)S(1)} %all_to_all.72), channel_id=1, replica_groups=mesh['h'=2,'u'=2,'p'=4,'c'=2] {'h','u','p','c'}, dimensions={0} | all-to-all | bytes 294912 | tf_op jit(solution)/shard_map/all_to_all | solution.py:48
  82.3 32.3 %all-to-all-done.2 = f32[16,2,1152]{2,1,0:T(2,128)S(1)} async-done(((f32[16,2,1152]{2,1,0:T(2,128)}), f32[16,2,1152]{2,1,0:T(2,128)S(1)}, u32[]{:S(2)}, u32[]{:S(2)}) %all-to-all-start.2) | async-done | bytes 147488 | tf_op jit(solution)/shard_map/all_to_all | solution.py:48
  137.9 36.3 %collective-permute-done.6 = bf16[768,576]{0,1:T(8,128)(2,1)} collective-permute-done((bf16[768,576]{0,1:T(8,128)(2,1)}, bf16[768,576]{0,1:T(8,128)(2,1)}, u32[]{:S(2)}, u32[]{:S(2)}) %collective-permute-start.6) | collective-permute-done | bytes 884768 | tf_op jit(solution)/shard_map/ppermute | solution.py:212
  208.3 5.6 convert_reduce_fusion
  215.8 11.2 %fusion.7 = bf16[1280,1536]{1,0:T(8,128)(2,1)} fusion(bf16[1280,1536]{1,0:T(8,128)(2,1)S(1)} %get-tuple-element.119, f32[1536]{0:T(1024)S(1)} %get-tuple-element.100, f32[1536]{0:T(1024)S(1)} %get-tuple-element.101, f32[1536]{0:T(1024)S(1)} %get-tuple-element.102, f32[1536]{0:T(1024)S(1)} %get-tuple-element.103, f32[1280]{0:T(1024)S(1)} %add_rsqrt_fusion, ...), kind=kLoop, calls=%fused_computation.9 | loop fusion | flops 17694720 | bytes 7900416 | tf_op jit(solution)/shard_map/convert_element_type | solution.py:355
  229.9 5.6 fusion.79
  240.5 15.7 %attention_forward.1 = (bf16[1280,192]{1,0:T(8,128)(2,1)}, f32[1280,3]{1,0:T(8,128)}) custom-call(s32[1]{0:T(128)} %dynamic_slice.112.length_ref, bf16[1280,576]{1,0:T(8,128)(2,1)} %pad_maximum_fusion.13.qkv_ref), custom_call_target="tpu_custom_call" | custom-call | flops 1258291200 | bytes 1966080 | tf_op jit(solution)/shard_map/attention_forward/pallas_call | solution.py:90
  265.4 8.4 all-to-all-done.4
  317.0 5.7 multiply_convert_fusion.1
  328.4 41.8 %all-gather.13.cloned.1.call-done = bf16[2560,1536]{1,0:T(8,128)(2,1)} async-done(((bf16[160,1536]{1,0:T(8,128)(2,1)}), bf16[2560,1536]{1,0:T(8,128)(2,1)}) %all-gather.13.cloned.1.call-update) | async-done | bytes 7864336 | tf_op jit(solution)/shard_map/all_gather | solution.py:430
  375.7 25.5 %collective-permute-done.10 = bf16[1536,384]{1,0:T(8,128)(2,1)} collective-permute-done((bf16[1536,384]{1,0:T(8,128)(2,1)}, bf16[1536,384]{1,0:T(8,128)(2,1)}, u32[]{:S(2)}, u32[]{:S(2)}) %collective-permute-start.10) | collective-permute-done | bytes 1179680 | tf_op jit(solution)/shard_map/ppermute | solution.py:365
  419.2 5.5 convolution_convert_fusion.1
  425.9 6.8 collective-permute-done.11
  473.1 14.7 %all-to-all-done.6 = bf16[8,160,1536]{2,1,0:T(8,128)(2,1)} async-done(((bf16[8,160,1536]{2,1,0:T(8,128)(2,1)}), bf16[8,160,1536]{2,1,0:T(8,128)(2,1)}, u32[]{:S(2)}, u32[]{:S(2)}) %all-to-all-start.6) | async-done | bytes 3932192 | tf_op jit(solution)/shard_map/all_to_all | solution.py:48
  512.6 7.3 all-to-all-start.7
  519.9 11.2 %all-to-all-done.7 = bf16[8,160,192]{2,1,0:T(8,128)(2,1)} async-done(((bf16[8,160,192]{2,1,0:T(8,128)(2,1)}), bf16[8,160,192]{2,1,0:T(8,128)(2,1)}, u32[]{:S(2)}, u32[]{:S(2)}) %all-to-all-start.7) | async-done | bytes 491552 | tf_op jit(solution)/shard_map/all_to_all | solution.py:48
  534.0 23.4 %attention_backward.1 = bf16[1280,576]{1,0:T(8,128)(2,1)} custom-call(s32[1]{0:T(128)} %dynamic_slice.112.length_ref, bf16[1280,576]{1,0:T(8,128)(2,1)} %pad_maximum_fusion.13.qkv_ref, bf16[1280,192]{1,0:T(8,128)(2,1)} %pad_maximum_fusion.22.grad_ref, f32[1280,3]{1,0:T(8,128)} %get-tuple-element.66.log_ref), custom_call_target="tpu_custom_call" | custom-call | flops 3145728000 | bytes 3440640 | tf_op jit(solution)/shard_map/attention_backward/pallas_call | solution.py:146
  566.0 7.7 reshape.335
  578.0 6.5 fusion.150
  589.4 8.7 fusion.140
  598.2 9.0 fusion.2
  638.2 8.6 all-to-all-start.9
  665.1 78.3 %collective-permute-done.14 = bf16[384,1536]{1,0:T(8,128)(2,1)} collective-permute-done((bf16[384,1536]{1,0:T(8,128)(2,1)}, bf16[384,1536]{1,0:T(8,128)(2,1)}, u32[]{:S(2)}, u32[]{:S(2)}) %collective-permute-start.14) | collective-permute-done | bytes 1179680 | tf_op jit(solution)/shard_map/ppermute | solution.py:463
  743.5 25.3 %collective-permute-done.15 = bf16[1536,384]{1,0:T(8,128)(2,1)} collective-permute-done((bf16[1536,384]{1,0:T(8,128)(2,1)}, bf16[1536,384]{1,0:T(8,128)(2,1)}, u32[]{:S(2)}, u32[]{:S(2)}) %collective-permute-start.15) | collective-permute-done | bytes 1179680 | tf_op jit(solution)/shard_map/ppermute | solution.py:464
  801.7 11.3 %collective-permute-done.21 = bf16[768,576]{0,1:T(8,128)(2,1)} collective-permute-done((bf16[768,576]{0,1:T(8,128)(2,1)}, bf16[768,576]{0,1:T(8,128)(2,1)}, u32[]{:S(2)}, u32[]{:S(2)}) %collective-permute-start.21) | collective-permute-done | bytes 884768 | tf_op jit(solution)/shard_map/ppermute | solution.py:221
  815.5 6.6 all-to-all-start.12
  825.4 11.0 %all-to-all-done.12 = bf16[32,2,576]{2,1,0:T(2,128)(2,1)S(1)} async-done(((bf16[32,2,576]{2,1,0:T(2,128)(2,1)}), bf16[32,2,576]{2,1,0:T(2,128)(2,1)S(1)}, u32[]{:S(2)}, u32[]{:S(2)}) %all-to-all-start.12) | async-done | bytes 73760 | tf_op jit(solution)/shard_map/all_to_all | solution.py:48
  859.7 7.8 all-to-all-done.10
  874.3 12.1 %all-to-all-done.14 = bf16[8,96,576]{2,1,0:T(8,128)(2,1)} async-done(((bf16[8,96,576]{2,1,0:T(8,128)(2,1)}), bf16[8,96,576]{2,1,0:T(8,128)(2,1)}, u32[]{:S(2)}, u32[]{:S(2)}) %all-to-all-start.14) | async-done | bytes 884768 | tf_op jit(solution)/shard_map/all_to_all | solution.py:48
  (498 shorter events, 418.1 us)
Async XLA Ops:
  7.2 181.5 %all-gather.7.cloned.1.call-start = ((), (), s32[]{:S(2)}) async-start(), calls=%async_computation.16 | async-start | bytes 3981312 | tf_op jit(solution)/shard_map/all_gather | solution.py:302
  7.9 270.6 %all-gather.9.cloned.1.call-start = ((), (), s32[]{:S(2)}) async-start(), calls=%async_computation.17 | async-start | bytes 9732096 | tf_op jit(solution)/shard_map/all_gather | solution.py:363
  14.9 24.0 %all-to-all-start.1 = ((bf16[8,96,576]{2,1,0:T(8,128)(2,1)}), bf16[8,96,576]{2,1,0:T(8,128)(2,1)S(1)}, u32[]{:S(2)}, u32[]{:S(2)}) async-start(bf16[8,96,576]{2,1,0:T(8,128)(2,1)} %copy.322), calls=%async_computation.1 | async-start | bytes 1966080 | tf_op jit(solution)/shard_map/all_to_all | solution.py:48
  20.2 270.8 %all-gather.11.cloned.1.call-start = ((), (), s32[]{:S(2)}) async-start(), calls=%async_computation.18 | async-start | bytes 7520256 | tf_op jit(solution)/shard_map/all_gather | solution.py:373
  40.2 27.7 %collective-permute-start.3 = (bf16[768,576]{0,1:T(8,128)(2,1)}, bf16[768,576]{0,1:T(8,128)(2,1)}, u32[]{:S(2)}, u32[]{:S(2)}) collective-permute-start(bf16[768,576]{0,1:T(8,128)(2,1)} %copy.323), channel_id=1, source_target_pairs={{8,0},{16,8},{24,16},{9,1},{17,9},{25,17},{10,2},{18,10},{26,18},{... | collective-permute-start | bytes 2654216 | tf_op jit(solution)/shard_map/ppermute | solution.py:213
  41.5 26.4 %collective-permute-start.2 = (bf16[768,576]{0,1:T(8,128)(2,1)}, bf16[768,576]{0,1:T(8,128)(2,1)}, u32[]{:S(2)}, u32[]{:S(2)}) collective-permute-start(bf16[768,576]{0,1:T(8,128)(2,1)} %copy.323), channel_id=1, source_target_pairs={{0,8},{8,16},{16,24},{1,9},{9,17},{17,25},{2,10},{10,18},{18,26},{... | collective-permute-start | bytes 2654216 | tf_op jit(solution)/shard_map/ppermute | solution.py:212
  67.9 51.2 %collective-permute-start.4 = (bf16[768,576]{0,1:T(8,128)(2,1)}, bf16[768,576]{0,1:T(8,128)(2,1)}, u32[]{:S(2)}, u32[]{:S(2)}) collective-permute-start(bf16[768,576]{0,1:T(8,128)(2,1)} %collective-permute-done.2), channel_id=1, source_target_pairs={{0,8},{8,16},{16,24},{1,9},{9,17},{17,25},{2,10},{10,18},{18,26},{... | collective-permute-start | bytes 2654216 | tf_op jit(solution)/shard_map/ppermute | solution.py:212
  72.6 46.5 %collective-permute-start.5 = (bf16[768,576]{0,1:T(8,128)(2,1)}, bf16[768,576]{0,1:T(8,128)(2,1)}, u32[]{:S(2)}, u32[]{:S(2)}) collective-permute-start(bf16[768,576]{0,1:T(8,128)(2,1)} %collective-permute-done.3), channel_id=1, source_target_pairs={{8,0},{16,8},{24,16},{9,1},{17,9},{25,17},{10,2},{18,10},{26,18},{... | collective-permute-start | bytes 2654216 | tf_op jit(solution)/shard_map/ppermute | solution.py:213
  74.6 40.0 %all-to-all-start.2 = ((f32[16,2,1152]{2,1,0:T(2,128)}), f32[16,2,1152]{2,1,0:T(2,128)S(1)}, u32[]{:S(2)}, u32[]{:S(2)}) async-start(f32[16,2,1152]{2,1,0:T(2,128)} %broadcast_in_dim.208), calls=%async_computation.2 | async-start | bytes 294912 | tf_op jit(solution)/shard_map/all_to_all | solution.py:48
  114.6 112.5 %all-to-all-start.3 = ((bf16[16,96,384]{2,1,0:T(8,128)(2,1)}), bf16[16,96,384]{2,1,0:T(8,128)(2,1)}, u32[]{:S(2)}, u32[]{:S(2)}) async-start(bf16[16,96,384]{2,1,0:T(8,128)(2,1)} %bitcast.237), calls=%async_computation.3 | async-start | bytes 2359296 | tf_op jit(solution)/shard_map/all_to_all | solution.py:48
  119.1 55.1 %collective-permute-start.6 = (bf16[768,576]{0,1:T(8,128)(2,1)}, bf16[768,576]{0,1:T(8,128)(2,1)}, u32[]{:S(2)}, u32[]{:S(2)}) collective-permute-start(bf16[768,576]{0,1:T(8,128)(2,1)} %collective-permute-done.4), channel_id=1, source_target_pairs={{0,8},{8,16},{16,24},{1,9},{9,17},{17,25},{2,10},{10,18},{18,26},{... | collective-permute-start | bytes 2654216 | tf_op jit(solution)/shard_map/ppermute | solution.py:212
  123.7 52.7 %collective-permute-start.7 = (bf16[768,576]{0,1:T(8,128)(2,1)}, bf16[768,576]{0,1:T(8,128)(2,1)}, u32[]{:S(2)}, u32[]{:S(2)}) collective-permute-start(bf16[768,576]{0,1:T(8,128)(2,1)} %collective-permute-done.5), channel_id=1, source_target_pairs={{8,0},{16,8},{24,16},{9,1},{17,9},{25,17},{10,2},{18,10},{26,18},{... | collective-permute-start | bytes 2654216 | tf_op jit(solution)/shard_map/ppermute | solution.py:213
  262.7 107.4 %all-gather.13.cloned.1.call-start = ((), (), s32[]{:S(2)}) async-start(), calls=%async_computation.19 | async-start | bytes 8355840 | tf_op jit(solution)/shard_map/all_gather | solution.py:430
  296.0 107.5 %collective-permute-start.9 = (bf16[384,1536]{1,0:T(8,128)(2,1)}, bf16[384,1536]{1,0:T(8,128)(2,1)}, u32[]{:S(2)}, u32[]{:S(2)}) collective-permute-start(bf16[384,1536]{1,0:T(8,128)(2,1)} %param.16), channel_id=1, source_target_pairs={{0,16},{16,0},{1,17},{17,1},{2,18},{18,2},{3,19},{19,3},{4,20},{20... | collective-permute-start | bytes 3538952 | tf_op jit(solution)/shard_map/ppermute | solution.py:366
  297.8 103.5 %collective-permute-start.10 = (bf16[1536,384]{1,0:T(8,128)(2,1)}, bf16[1536,384]{1,0:T(8,128)(2,1)}, u32[]{:S(2)}, u32[]{:S(2)}) collective-permute-start(bf16[1536,384]{1,0:T(8,128)(2,1)} %bitcast.19), channel_id=1, source_target_pairs={{0,16},{16,0},{1,17},{17,1},{2,18},{18,2},{3,19},{19,3},{4,20},{20... | collective-permute-start | bytes 3538952 | tf_op jit(solution)/shard_map/ppermute | solution.py:365
  435.6 52.2 %all-to-all-start.6 = ((bf16[8,160,1536]{2,1,0:T(8,128)(2,1)}), bf16[8,160,1536]{2,1,0:T(8,128)(2,1)}, u32[]{:S(2)}, u32[]{:S(2)}) async-start(bf16[8,160,1536]{2,1,0:T(8,128)(2,1)} %fusion.13), calls=%async_computation.6 | async-start | bytes 7864320 | tf_op jit(solution)/shard_map/all_to_all | solution.py:48
  519.9 248.9 %all-gather.15.cloned.1.call-start = ((), (), s32[]{:S(2)}) async-start(), calls=%async_computation.20 | async-start | bytes 4423680 | tf_op jit(solution)/shard_map/all_gather | solution.py:479
  584.6 53.6 %all-to-all-start.8 = ((bf16[8,160,1536]{2,1,0:T(8,128)(2,1)}), bf16[8,160,1536]{2,1,0:T(8,128)(2,1)}, u32[]{:S(2)}, u32[]{:S(2)}) async-start(bf16[8,160,1536]{2,1,0:T(8,128)(2,1)} %fusion.12), calls=%async_computation.8 | async-start | bytes 7864320 | tf_op jit(solution)/shard_map/all_to_all | solution.py:48
  624.9 118.6 %collective-permute-start.14 = (bf16[384,1536]{1,0:T(8,128)(2,1)}, bf16[384,1536]{1,0:T(8,128)(2,1)}, u32[]{:S(2)}, u32[]{:S(2)}) collective-permute-start(bf16[384,1536]{1,0:T(8,128)(2,1)} %get-tuple-element.71), channel_id=1, source_target_pairs={{0,16},{16,0},{1,17},{17,1},{2,18},{18,2},{3,19},{19,3},{4,20},{20... | collective-permute-start | bytes 3538952 | tf_op jit(solution)/shard_map/ppermute | solution.py:463
  626.7 142.1 %collective-permute-start.15 = (bf16[1536,384]{1,0:T(8,128)(2,1)}, bf16[1536,384]{1,0:T(8,128)(2,1)}, u32[]{:S(2)}, u32[]{:S(2)}) collective-permute-start(bf16[1536,384]{1,0:T(8,128)(2,1)} %get-tuple-element.72), channel_id=1, source_target_pairs={{0,16},{16,0},{1,17},{17,1},{2,18},{18,2},{3,19},{19,3},{4,20},{20... | collective-permute-start | bytes 3538952 | tf_op jit(solution)/shard_map/ppermute | solution.py:464
  638.2 130.6 %all-to-all-start.9 = ((bf16[4,160,1536]{2,1,0:T(8,128)(2,1)}), bf16[4,160,1536]{2,1,0:T(8,128)(2,1)}, u32[]{:S(2)}, u32[]{:S(2)}) async-start(bf16[4,160,1536]{2,1,0:T(8,128)(2,1)} %fusion.37), calls=%async_computation.9 | async-start | bytes 3932160 | tf_op jit(solution)/shard_map/all_to_all | solution.py:48
  646.8 255.1 %all-gather.17.cloned.1.call-start = ((), (), s32[]{:S(2)}) async-start(), calls=%async_computation.21 | async-start | bytes 4423680 | tf_op jit(solution)/shard_map/all_gather | solution.py:533
  656.2 142.5 %collective-permute-start.22 = (bf16[768,576]{0,1:T(8,128)(2,1)}, bf16[768,576]{0,1:T(8,128)(2,1)}, u32[]{:S(2)}, u32[]{:S(2)}) collective-permute-start(bf16[768,576]{0,1:T(8,128)(2,1)} %get-tuple-element.130), channel_id=1, source_target_pairs={{0,24},{8,0},{16,8},{24,16},{1,25},{9,1},{17,9},{25,17},{2,26},{10... | collective-permute-start | bytes 2654216 | tf_op jit(solution)/shard_map/ppermute | solution.py:221
  658.3 154.8 %collective-permute-start.21 = (bf16[768,576]{0,1:T(8,128)(2,1)}, bf16[768,576]{0,1:T(8,128)(2,1)}, u32[]{:S(2)}, u32[]{:S(2)}) collective-permute-start(bf16[768,576]{0,1:T(8,128)(2,1)} %get-tuple-element.131), channel_id=1, source_target_pairs={{0,16},{8,24},{16,0},{24,8},{1,17},{9,25},{17,1},{25,9},{2,18},{10... | collective-permute-start | bytes 2654216 | tf_op jit(solution)/shard_map/ppermute | solution.py:221
  658.3 154.8 %collective-permute-start.20 = (bf16[768,576]{0,1:T(8,128)(2,1)}, bf16[768,576]{0,1:T(8,128)(2,1)}, u32[]{:S(2)}, u32[]{:S(2)}) collective-permute-start(bf16[768,576]{0,1:T(8,128)(2,1)} %get-tuple-element.132), channel_id=1, source_target_pairs={{0,8},{8,16},{16,24},{24,0},{1,9},{9,17},{17,25},{25,1},{2,10},{10... | collective-permute-start | bytes 2654216 | tf_op jit(solution)/shard_map/ppermute | solution.py:221
  778.2 35.3 %all-to-all-start.11 = ((f32[8,2,1152]{2,1,0:T(2,128)}), f32[8,2,1152]{2,1,0:T(2,128)S(1)}, u32[]{:S(2)}, u32[]{:S(2)}) async-start(f32[8,2,1152]{2,1,0:T(2,128)} %copy.356), calls=%async_computation.11 | async-start | bytes 147456 | tf_op jit(solution)/shard_map/all_to_all | solution.py:48
  784.5 28.6 %collective-permute-start.19 = (f32[8,1536]{1,0:T(8,128)S(1)}, f32[8,1536]{1,0:T(8,128)S(1)}, u32[]{:S(2)}, u32[]{:S(2)}) collective-permute-start(f32[8,1536]{1,0:T(8,128)S(1)} %get-tuple-element.141), channel_id=1, source_target_pairs={{0,8},{8,16},{16,24},{1,9},{9,17},{17,25},{2,10},{10,18},{18,26},{... | collective-permute-start | bytes 147464 | tf_op jit(solution)/shard_map/ppermute | solution.py:524
  786.4 27.1 %collective-permute-start.18 = (f32[8,1536]{1,0:T(8,128)S(1)}, f32[8,1536]{1,0:T(8,128)S(1)}, u32[]{:S(2)}, u32[]{:S(2)}) collective-permute-start(f32[8,1536]{1,0:T(8,128)S(1)} %get-tuple-element.142), channel_id=1, source_target_pairs={{8,0},{16,8},{24,16},{9,1},{17,9},{25,17},{10,2},{18,10},{26,18},{... | collective-permute-start | bytes 147464 | tf_op jit(solution)/shard_map/ppermute | solution.py:523
  798.7 58.7 %collective-permute-start.23 = (bf16[96,1536]{1,0:T(8,128)(2,1)}, bf16[96,1536]{1,0:T(8,128)(2,1)}, u32[]{:S(2)}, u32[]{:S(2)}) collective-permute-start(bf16[96,1536]{1,0:T(8,128)(2,1)} %get-tuple-element.136), channel_id=1, source_target_pairs={{0,8},{8,16},{16,24},{24,0},{1,9},{9,17},{17,25},{25,1},{2,10},{10... | collective-permute-start | bytes 884744 | tf_op jit(solution)/shard_map/ppermute | solution.py:221
  813.0 44.4 %collective-permute-start.25 = (bf16[96,1536]{1,0:T(8,128)(2,1)}, bf16[96,1536]{1,0:T(8,128)(2,1)}, u32[]{:S(2)}, u32[]{:S(2)}) collective-permute-start(bf16[96,1536]{1,0:T(8,128)(2,1)} %get-tuple-element.137), channel_id=1, source_target_pairs={{0,24},{8,0},{16,8},{24,16},{1,25},{9,1},{17,9},{25,17},{2,26},{10... | collective-permute-start | bytes 884744 | tf_op jit(solution)/shard_map/ppermute | solution.py:221
  813.0 44.4 %collective-permute-start.24 = (bf16[96,1536]{1,0:T(8,128)(2,1)}, bf16[96,1536]{1,0:T(8,128)(2,1)}, u32[]{:S(2)}, u32[]{:S(2)}) collective-permute-start(bf16[96,1536]{1,0:T(8,128)(2,1)} %get-tuple-element.138), channel_id=1, source_target_pairs={{0,16},{8,24},{16,0},{24,8},{1,17},{9,25},{17,1},{25,9},{2,18},{10... | collective-permute-start | bytes 884744 | tf_op jit(solution)/shard_map/ppermute | solution.py:221
  886.4 31.1 %all-to-all-start.15 = ((bf16[16,96,384]{2,1,0:T(8,128)(2,1)}), bf16[16,96,384]{2,1,0:T(8,128)(2,1)}, u32[]{:S(2)}, u32[]{:S(2)}) async-start(bf16[16,96,384]{2,1,0:T(8,128)(2,1)} %bitcast.234), calls=%async_computation.15 | async-start | bytes 2359296 | tf_op jit(solution)/shard_map/all_to_all | solution.py:48
  (116 other events, 1411.7 us)
Sparse Core Ops, SparseCore 0:
  9.9 46.6 all-gather.6
  59.4 107.7 all-gather.8
  168.8 52.4 all-gather.10
  288.8 81.3 all-gather.12
  584.7 75.8 all-gather.14
  773.8 36.9 all-gather.16
